TPU v7x, 128 devices: a whole 4x4x4 slice. The times are simulated.
128 devices in a mesh: dp: 1, sp: 128 (over z, y, x, core).
Axes of the slice: x: 4, y: 4, z: 4, core: 2. Of those that a mesh axis runs over, the one named last changes fastest.
Arguments:
- x_in: bfloat16 [4096, 3584], P(('dp', 'sp'))
- seg_id: int32 [4096], P(('dp', 'sp'))
- pos_id: int32 [4096], P(('dp', 'sp'))
- w_dq: bfloat16 [3584, 768], replicated
- g_q: bfloat16 [768], replicated
- w_uq: bfloat16 [768, 24576], replicated
- w_dkv: bfloat16 [3584, 576], replicated
- g_kv: bfloat16 [512], replicated
- w_ukv: bfloat16 [512, 32768], replicated
- w_o: bfloat16 [16384, 3584], replicated
- g_ffn: bfloat16 [3584], replicated
- w_gate: bfloat16 [3584, 9216], P(None, 'sp')
- w_up: bfloat16 [3584, 9216], P(None, 'sp')
- w_down: bfloat16 [9216, 3584], P('sp')
Outputs:
- output: bfloat16 [4096, 3584], P(('dp', 'sp'))
All inputs are finite; a program needn't handle non-finite values.
Results may differ from a plain program's by a relative error of at most 0.0161625.
Values are sent between devices in bfloat16 or wider.
A program may use at most 1 GiB of HBM per device.

v0:
```python
import jax
import jax.numpy as jnp
from jax import lax
from jax.sharding import PartitionSpec as P

NOPE_DIM = 128
ROPE_DIM = 64
VALUE_DIM = 128
KV_LATENT = 512
QK_DIM = NOPE_DIM + ROPE_DIM
KV_DIM = NOPE_DIM + VALUE_DIM
SCORE_SCALE = QK_DIM ** -0.5


def rms_norm(vec_in, gain_vec):
    mean_sq = jnp.mean(vec_in * vec_in, axis=-1, keepdims=True)
    return vec_in * lax.rsqrt(mean_sq + 1e-6) * gain_vec.astype(jnp.float32)


def apply_rope(vec_in, positions):
    half_dim = ROPE_DIM // 2
    inv_freq = 10000.0 ** (-jnp.arange(half_dim, dtype=jnp.float32) / half_dim)
    angles = positions.astype(jnp.float32)[..., None] * inv_freq
    cosine = jnp.cos(angles)
    sine_v = jnp.sin(angles)
    lo_half = vec_in[..., :half_dim]
    hi_half = vec_in[..., half_dim:]
    return jnp.concatenate([lo_half * cosine - hi_half * sine_v, hi_half * cosine + lo_half * sine_v], axis=-1)


def latents(x_rows, pos_rows, w_dq, g_q, w_dkv, g_kv):
    q_lin = jnp.dot(x_rows, w_dq, preferred_element_type=jnp.float32)
    c_q = rms_norm(q_lin, g_q).astype(jnp.bfloat16)
    kv_lin = jnp.dot(x_rows, w_dkv, preferred_element_type=jnp.float32)
    c_kv = rms_norm(kv_lin[:, :KV_LATENT], g_kv).astype(jnp.bfloat16)
    k_rope = apply_rope(kv_lin[:, KV_LATENT:], pos_rows).astype(jnp.bfloat16)
    return c_q, c_kv, k_rope


def ffn_partial(h_all, w_gate, w_up, w_down):
    gate_lin = jnp.dot(h_all, w_gate, preferred_element_type=jnp.float32)
    up_lin = jnp.dot(h_all, w_up, preferred_element_type=jnp.float32)
    act_val = (jax.nn.silu(gate_lin) * up_lin).astype(jnp.bfloat16)
    return jnp.dot(act_val, w_down, preferred_element_type=jnp.float32)


def solution(mesh):
    group_size = mesh.shape['sp']
    tok_spec = P(('dp', 'sp'), None)
    row_spec = P(('dp', 'sp'))
    full_spec = P()
    col_spec = P(None, 'sp')

    def device_fn(x_blk, seg_blk, pos_blk, w_dq, g_q, w_uq, w_dkv, g_kv, w_ukv, w_o, g_ffn, w_gate, w_up, w_down):
        blk_len = x_blk.shape[0]
        tok_total = blk_len * group_size
        heads_loc = w_uq.shape[1] // QK_DIM
        q_block = min(tok_total, 128)
        n_qblk = tok_total // q_block
        c_q, c_kv, k_rope = latents(x_blk, pos_blk, w_dq, g_q, w_dkv, g_kv)
        cq_all = lax.all_gather(c_q, 'sp', axis=0, tiled=True)
        ckv_all = lax.all_gather(c_kv, 'sp', axis=0, tiled=True)
        kr_all = lax.all_gather(k_rope, 'sp', axis=0, tiled=True)
        seg_all = lax.all_gather(seg_blk, 'sp', axis=0, tiled=True)
        pos_all = lax.all_gather(pos_blk, 'sp', axis=0, tiled=True)
        q_lin = jnp.dot(cq_all, w_uq, preferred_element_type=jnp.float32).reshape(tok_total, heads_loc, QK_DIM)
        q_nope = q_lin[..., :NOPE_DIM].astype(jnp.bfloat16)
        q_rope = apply_rope(q_lin[..., NOPE_DIM:], pos_all[:, None]).astype(jnp.bfloat16)
        kv_up = jnp.dot(ckv_all, w_ukv, preferred_element_type=jnp.float32).astype(jnp.bfloat16).reshape(tok_total, heads_loc, KV_DIM)
        k_nope = kv_up[..., :NOPE_DIM]
        v_heads = kv_up[..., NOPE_DIM:]

        def attend(blk_idx):
            row_begin = blk_idx * q_block
            qn_blk = lax.dynamic_slice_in_dim(q_nope, row_begin, q_block, axis=0)
            qr_blk = lax.dynamic_slice_in_dim(q_rope, row_begin, q_block, axis=0)
            seg_q = lax.dynamic_slice_in_dim(seg_all, row_begin, q_block)
            pos_q = lax.dynamic_slice_in_dim(pos_all, row_begin, q_block)
            scores = jnp.einsum('qhd,khd->qhk', qn_blk, k_nope, preferred_element_type=jnp.float32)
            scores = scores + jnp.einsum('qhr,kr->qhk', qr_blk, kr_all, preferred_element_type=jnp.float32)
            allowed = (seg_q[:, None] == seg_all[None, :]) & (pos_all[None, :] <= pos_q[:, None])
            scores = jnp.where(allowed[:, None, :], scores * SCORE_SCALE, -jnp.inf)
            row_peak = jnp.max(scores, axis=-1, keepdims=True)
            prob_w = jnp.exp(scores - row_peak)
            row_total = jnp.sum(prob_w, axis=-1)
            head_out = jnp.einsum('qhk,khd->qhd', prob_w.astype(jnp.bfloat16), v_heads, preferred_element_type=jnp.float32)
            return (head_out / row_total[..., None]).astype(jnp.bfloat16)

        o_heads = lax.map(attend, jnp.arange(n_qblk))
        o_loc = o_heads.reshape(tok_total, heads_loc * VALUE_DIM)
        o_tok = lax.all_to_all(o_loc, 'sp', 0, 1, tiled=True)
        y_att = jnp.dot(o_tok, w_o, preferred_element_type=jnp.float32).astype(jnp.bfloat16)
        h_loc = rms_norm(y_att.astype(jnp.float32), g_ffn).astype(jnp.bfloat16)
        h_all = lax.all_gather(h_loc, 'sp', axis=0, tiled=True)
        part_sum = ffn_partial(h_all, w_gate, w_up, w_down)
        ffn_out = lax.psum_scatter(part_sum, 'sp', scatter_dimension=0, tiled=True)
        return (y_att.astype(jnp.float32) + ffn_out).astype(jnp.bfloat16)

    return jax.shard_map(device_fn, mesh=mesh, in_specs=(tok_spec, row_spec, row_spec, full_spec, full_spec, col_spec, full_spec, full_spec, col_spec, full_spec, full_spec, col_spec, col_spec, P('sp', None)), out_specs=tok_spec, check_vma=False)
```

profile of v0, /device:TPU:0, one launch (start us, length us, event | category | flops | bytes accessed | tf_op | source)
XLA Modules:
  0.0 1280.6 jit_solution(548668226578978988)
XLA Ops:
  7.3 3.6 fusion.55
  11.8 3.7 multiply_reduce_fusion.1
  16.9 68.4 %all-reduce.2 = (s32[4096]{0:T(1024)S(1)}, s32[4096]{0:T(1024)S(1)}) all-reduce(s32[4096]{0:T(1024)S(1)} %dynamic-update-slice, s32[4096]{0:T(1024)S(1)} %dynamic-update-slice.1), channel_id=1, replica_groups=mesh['dp'=1,'sp'=128] {'sp'}, use_global_device_ids=true, to_apply=%add | all-reduce | flops 8192 | bytes 65536
  85.5 34.1 %all_gather.22 = bf16[4096,64]{1,0:T(8,128)(2,1)S(1)} all-gather(bf16[32,64]{1,0:T(8,128)(2,1)S(1)} %pad_maximum_fusion.1), channel_id=1, replica_groups=mesh['dp'=1,'sp'=128] {'sp'}, dimensions={0}, use_global_device_ids=true | all-gather | bytes 528384 | tf_op jit(solution)/shard_map/all_gather | solution.py:63
  119.6 3.5 fusion.20
  124.2 25.6 %all-gather.4.cloned.1.call-done = bf16[4096,768]{1,0:T(8,128)(2,1)} async-done(((bf16[32,768]{1,0:T(8,128)(2,1)}), bf16[4096,768]{1,0:T(8,128)(2,1)}) %all-gather.4.cloned.1.call-update) | async-done | bytes 6291472 | tf_op jit(solution)/shard_map/all_gather | solution.py:61
  149.8 5.1 convolution_bitcast_fusion.3
  156.1 2.3 fusion.37
  158.4 167.2 %while.10 = (s32[]{:T(128)}, bf16[32,128,1,128]{3,1,2,0:T(8,128)(2,1)}, s32[32]{0:T(128)S(1)}, s32[4096]{0:T(1024)S(1)}, s32[4096]{0:T(1024)S(1)}, /*index=5*/bf...) while((s32[]{:T(128)}, ...), condition=%wide.region_5.6_spmd, body=%wide.region_2.5_spmd.sunk | while | flops 341344000 | bytes 17946360 | solution.py:89
  160.3 1.7 fusion.82
  162.5 1.2 fusion.84
  165.5 1.7 fusion.82
  170.8 1.7 fusion.82
  173.0 1.2 fusion.84
  176.0 1.7 fusion.82
  181.2 1.7 fusion.82
  186.4 1.7 fusion.82
  188.6 1.2 fusion.84
  191.7 1.7 fusion.82
  196.9 1.7 fusion.82
  202.1 1.7 fusion.82
  204.3 1.2 fusion.84
  207.3 1.7 fusion.82
  212.5 1.7 fusion.82
  214.7 1.2 fusion.84
  217.8 1.7 fusion.82
  220.0 1.1 fusion.84
  223.0 1.7 fusion.82
  225.2 1.2 fusion.84
  228.2 1.7 fusion.82
  230.4 1.2 fusion.84
  233.5 1.7 fusion.82
  235.6 1.2 fusion.84
  238.7 1.7 fusion.82
  243.9 1.7 fusion.82
  246.1 1.2 fusion.84
  249.1 1.7 fusion.82
  254.4 1.7 fusion.82
  256.6 1.1 fusion.84
  259.6 1.7 fusion.82
  264.8 1.7 fusion.82
  270.0 1.7 fusion.82
  275.2 1.7 fusion.82
  280.5 1.7 fusion.82
  282.7 1.2 fusion.84
  285.7 1.7 fusion.82
  290.9 1.7 fusion.82
  296.1 1.7 fusion.82
  298.3 1.2 fusion.84
  301.3 1.7 fusion.82
  303.5 1.2 fusion.84
  306.6 1.7 fusion.82
  311.8 1.7 fusion.82
  317.0 1.7 fusion.82
  319.2 1.2 fusion.84
  322.2 1.7 fusion.82
  325.6 6.1 all-to-all-start
  331.8 18.8 %all-to-all-done = bf16[128,32,128]{2,1,0:T(8,128)(2,1)S(1)} async-done(((bf16[128,32,128]{2,1,0:T(8,128)(2,1)}), bf16[128,32,128]{2,1,0:T(8,128)(2,1)S(1)}, u32[]{:S(2)}, u32[]{:S(2)}) %all-to-all-start) | async-done | bytes 1048608 | tf_op jit(solution)/shard_map/all_to_all | solution.py:91
  350.6 39.0 %multiply_reduce_fusion = (f32[32]{0:T(128)S(1)}, f32[32,3584]{1,0:T(8,128)S(1)}) fusion(bf16[16384,3584]{1,0:T(8,128)(2,1)} %param.25, bf16[128,32,128]{2,1,0:T(8,128)(2,1)S(1)} %all-to-all-done), kind=kOutput, calls=%fused_computation.53 | convolution fusion | flops 3758555136 | bytes 118947968 | tf_op jit(solution)/shard_map/dot_general | solution.py:92
  390.5 95.5 %all-gather.8.cloned.1.call-done = bf16[4096,3584]{1,0:T(8,128)(2,1)} async-done(((bf16[32,3584]{1,0:T(8,128)(2,1)}), bf16[4096,3584]{1,0:T(8,128)(2,1)}) %all-gather.8.cloned.1.call-update) | async-done | bytes 29360144 | tf_op jit(solution)/shard_map/all_gather | solution.py:94
  486.0 14.2 %fusion.56 = f32[4096,72]{0,1:T(8,128)S(1)} fusion(bf16[4096,3584]{1,0:T(8,128)(2,1)} %all-gather.8.cloned.1.call-done, bf16[3584,72]{0,1:T(8,128)(2,1)S(1)} %copy-done.4), kind=kOutput, calls=%fused_computation.81 | convolution fusion | flops 2113929216 | bytes 31055872 | tf_op jit(solution)/shard_map/dot_general | solution.py:41
  500.2 32.3 %fusion.22 = f32[4096,3584]{1,0:T(8,128)} fusion(bf16[72,3584]{1,0:T(8,128)(2,1)S(1)} %copy-done, bf16[4096,3584]{1,0:T(8,128)(2,1)} %all-gather.8.cloned.1.call-done, bf16[3584,72]{0,1:T(8,128)(2,1)S(1)} %copy-done.2, f32[4096,72]{0,1:T(8,128)S(1)} %fusion.56), kind=kOutput, calls=%fused_computation.28 | convolution fusion | flops 4229627904 | bytes 90292224 | tf_op jit(solution)/shard_map/dot_general | solution.py:44
  532.6 739.8 %reduce-scatter.2.cloned.1.call-done = f32[32,3584]{1,0:T(8,128)} async-done(((f32[4096,3584]{1,0:T(8,128)}), f32[32,3584]{1,0:T(8,128)}) %reduce-scatter.2.cloned.1.call-update) | async-done | bytes 458768 | tf_op jit(solution)/shard_map/reduce_scatter | solution.py:96
  1272.3 1.7 add_convert_fusion
  (290 shorter events, 78.9 us)
Async XLA Ops:
  6.5 493.7 %copy-start = (bf16[72,3584]{1,0:T(8,128)(2,1)S(1)}, bf16[72,3584]{1,0:T(8,128)(2,1)}, u32[]{:S(2)}) copy-start(bf16[72,3584]{1,0:T(8,128)(2,1)} %param.29) | copy-start | bytes 1548292
  6.5 5.3 copy-start.3
  6.5 5.3 copy-start.6
  6.5 113.1 %all-gather.6.cloned.1.call-start = ((), (), s32[]{:S(2)}) async-start(), calls=%async_computation.3 | async-start | bytes 4227072 | tf_op jit(solution)/shard_map/all_gather | solution.py:62
  10.9 5.5 copy-start.7
  10.9 5.8 copy-start.8
  11.8 138.1 %all-gather.4.cloned.1.call-start = ((), (), s32[]{:S(2)}) async-start(), calls=%async_computation.2 | async-start | bytes 6340608 | tf_op jit(solution)/shard_map/all_gather | solution.py:61
  158.4 173.3 %copy-start.5 = (bf16[3584]{0:T(1024)(128)(2,1)S(1)}, bf16[3584]{0:T(1024)(128)(2,1)}, u32[]{:S(2)}) copy-start(bf16[3584]{0:T(1024)(128)(2,1)} %param.26) | copy-start | bytes 21508
  160.3 2.2 copy-start.1
  165.5 2.2 copy-start.1
  170.8 2.2 copy-start.1
  176.0 2.2 copy-start.1
  181.2 2.2 copy-start.1
  186.4 2.2 copy-start.1
  191.6 2.2 copy-start.1
  196.9 2.2 copy-start.1
  202.1 2.2 copy-start.1
  207.3 2.2 copy-start.1
  212.5 2.2 copy-start.1
  217.8 2.2 copy-start.1
  223.0 2.2 copy-start.1
  228.2 2.2 copy-start.1
  233.4 2.2 copy-start.1
  238.7 2.2 copy-start.1
  243.9 2.2 copy-start.1
  249.1 2.2 copy-start.1
  254.3 2.2 copy-start.1
  259.6 2.2 copy-start.1
  264.8 2.2 copy-start.1
  270.0 2.2 copy-start.1
  275.2 2.2 copy-start.1
  280.4 2.2 copy-start.1
  285.7 2.2 copy-start.1
  290.9 2.2 copy-start.1
  296.1 2.2 copy-start.1
  301.3 2.2 copy-start.1
  306.6 2.2 copy-start.1
  311.8 2.2 copy-start.1
  317.0 2.2 copy-start.1
  322.2 2.2 copy-start.1
  325.6 25.0 %all-to-all-start = ((bf16[128,32,128]{2,1,0:T(8,128)(2,1)}), bf16[128,32,128]{2,1,0:T(8,128)(2,1)S(1)}, u32[]{:S(2)}, u32[]{:S(2)}) async-start(bf16[128,32,128]{2,1,0:T(8,128)(2,1)} %bitcast.101), calls=%async_computation | async-start | bytes 2097152 | tf_op jit(solution)/shard_map/all_to_all | solution.py:91
  331.7 154.3 %all-gather.8.cloned.1.call-start = ((), (), s32[]{:S(2)}) async-start(), calls=%async_computation.4 | async-start | bytes 29589504 | tf_op jit(solution)/shard_map/all_gather | solution.py:94
  331.8 154.2 %copy-start.4 = (bf16[3584,72]{0,1:T(8,128)(2,1)S(1)}, bf16[3584,72]{0,1:T(8,128)(2,1)}, u32[]{:S(2)}) copy-start(bf16[3584,72]{0,1:T(8,128)(2,1)} %param.27) | copy-start | bytes 1548292
  390.5 109.7 %copy-start.2 = (bf16[3584,72]{0,1:T(8,128)(2,1)S(1)}, bf16[3584,72]{0,1:T(8,128)(2,1)}, u32[]{:S(2)}) copy-start(bf16[3584,72]{0,1:T(8,128)(2,1)} %param.28) | copy-start | bytes 1548292
  390.5 881.9 %reduce-scatter.2.cloned.1.call-start = ((), (), s32[]{:S(2)}) async-start(), calls=%async_computation.5 | async-start | bytes 59179008 | tf_op jit(solution)/shard_map/reduce_scatter | solution.py:96
Sparse Core Ops, SparseCore 0:
  11.9 69.0 all-gather.5
  84.1 65.6 all-gather.3
  390.6 95.3 all-gather.7
  532.7 739.6 reduce-scatter.1
where the time goes:
time: 1280 us
  waiting for transfers between devices  880 us (69%)
  matrix products  209 us (16%)
  blocking collectives  102 us (8%)
  local copies, waits for them, and re-layouts  26.5 us (2%)
  other arithmetic  21.7 us (2%)
  loops' own time  21.6 us (2%)
  between operations  13.4 us (1%)
    reduce_scatter x1, waiting for transfers between devices, device_fn(): ffn_out = lax.psum_scatter(part_sum, 'sp', scatter_dimension=0, tiled=True)  740 us
    all_gather x1, waiting for transfers between devices, device_fn(): h_all = lax.all_gather(h_loc, 'sp', axis=0, tiled=True)  95.5 us
    unnamed x1, blocking collectives  68.4 us
    dot_general x32, matrix products, attend(): jnp.einsum('qhd,khd->qhk', qn_blk, k_nope, preferred_element_type=jnp.flo...  55.8 us
    dot_general x1, matrix products, device_fn(): jnp.dot(o_tok, w_o, preferred_element_type=jnp.float32).astype(jnp.bfloat16)  39 us
    dot_general x32, matrix products, attend(): jnp.einsum('qhk,khd->qhd', prob_w.astype(jnp.bfloat16), v_heads, preferre...  36.7 us
    all_gather x1, blocking collectives, device_fn(): kr_all = lax.all_gather(k_rope, 'sp', axis=0, tiled=True)  34.1 us
    dot_general x1, matrix products, ffn_partial(): return jnp.dot(act_val, w_down, preferred_element_type=jnp.float32)  32.3 us
  transfers between devices with their start and end apart: 5, of which 4 were waited for; matrix products, arithmetic and copies ran while one was open for 1% of the time, Pallas kernels for 0%

commit v1 on v0

v1 whole, which is shorter than its diff:
```python
import functools

import jax
import jax.numpy as jnp
from jax import lax
from jax.experimental import pallas as pl
from jax.experimental.pallas import tpu as pltpu
from jax.sharding import PartitionSpec as P

NOPE_DIM = 128
ROPE_DIM = 64
VALUE_DIM = 128
KV_LATENT = 512
QK_DIM = NOPE_DIM + ROPE_DIM
KV_DIM = NOPE_DIM + VALUE_DIM
SCORE_SCALE = QK_DIM ** -0.5
LOG2E = 1.4426950408889634
MASKED = -0.7 * 3.4028234663852886e38

RING = 4
CORES = 2


def rms_norm(vec_in, gain_vec):
    mean_sq = jnp.mean(vec_in * vec_in, axis=-1, keepdims=True)
    return vec_in * lax.rsqrt(mean_sq + 1e-6) * gain_vec.astype(jnp.float32)


def rope_angles(positions):
    half_dim = ROPE_DIM // 2
    inv_freq = 10000.0 ** (-jnp.arange(half_dim, dtype=jnp.float32) / half_dim)
    return positions.astype(jnp.float32)[..., None] * inv_freq


def apply_rope(vec_in, positions):
    half_dim = ROPE_DIM // 2
    angles = rope_angles(positions)
    cosine = jnp.cos(angles)
    sine_v = jnp.sin(angles)
    lo_half = vec_in[..., :half_dim]
    hi_half = vec_in[..., half_dim:]
    return jnp.concatenate([lo_half * cosine - hi_half * sine_v, hi_half * cosine + lo_half * sine_v], axis=-1)


def attn_kernel(lo_ref, clear_ref, cq_ref, kv_ref, wq_ref, wk_ref, wv_ref, cos_ref, sin_ref, start_ref, pos_ref,
                o_ref, k_buf, v_buf, q_buf, acc_ref, *, blk, n_blk):
    i = pl.program_id(0)
    half = ROPE_DIM // 2
    nt = (((1,), (1,)), ((), ()))

    @pl.when(i == 0)
    def _():
        @pl.loop(0, n_blk)
        def _(b):
            rows = pl.ds(pl.multiple_of(b * blk, blk), blk)
            lat = kv_ref[rows, :KV_LATENT]
            k_buf[rows, :NOPE_DIM] = jnp.dot(lat, wk_ref[...], preferred_element_type=jnp.float32).astype(jnp.bfloat16)
            k_buf[rows, NOPE_DIM:] = kv_ref[rows, KV_LATENT:]
            v_buf[:, rows] = lax.dot_general(wv_ref[...], lat, nt, preferred_element_type=jnp.float32).astype(jnp.bfloat16)
        q_buf[QK_DIM:, :] = jnp.zeros((2 * NOPE_DIM - QK_DIM, blk), jnp.bfloat16)

    qt = lax.dot_general(wq_ref[...], cq_ref[...], nt, preferred_element_type=jnp.float32)
    q_buf[:NOPE_DIM, :] = qt[:NOPE_DIM].astype(jnp.bfloat16)
    lo_half = qt[NOPE_DIM:NOPE_DIM + half]
    hi_half = qt[NOPE_DIM + half:]
    q_buf[NOPE_DIM:NOPE_DIM + half, :] = (lo_half * cos_ref[...] - hi_half * sin_ref[...]).astype(jnp.bfloat16)
    q_buf[NOPE_DIM + half:QK_DIM, :] = (hi_half * cos_ref[...] + lo_half * sin_ref[...]).astype(jnp.bfloat16)
    acc_ref[...] = jnp.zeros_like(acc_ref)

    def block(masked, kb, carry):
        m_old, l_old = carry
        rows = pl.ds(pl.multiple_of(kb * blk, blk), blk)
        s = jnp.dot(k_buf[rows, :], q_buf[...], preferred_element_type=jnp.float32)
        if masked:
            key = kb * blk + lax.broadcasted_iota(jnp.int32, s.shape, 0)
            back = key - start_ref[...]
            s = jnp.where((back >= 0) & (back <= pos_ref[...]), s, MASKED)
        m_new = jnp.maximum(m_old, jnp.max(s, axis=0, keepdims=True))
        p = jnp.exp2((s - m_new) * (SCORE_SCALE * LOG2E))
        alpha = jnp.exp2((m_old - m_new) * (SCORE_SCALE * LOG2E))
        l_new = l_old * alpha + jnp.sum(p, axis=0, keepdims=True)
        acc_ref[...] = acc_ref[...] * alpha + jnp.dot(v_buf[:, rows], p.astype(jnp.bfloat16), preferred_element_type=jnp.float32)
        return m_new, l_new

    carry = (jnp.full((1, blk), MASKED, jnp.float32), jnp.zeros((1, blk), jnp.float32))
    lo = lo_ref[i]
    clear = clear_ref[i]
    carry = lax.fori_loop(lo, clear, functools.partial(block, True), carry)
    carry = lax.fori_loop(clear, i, functools.partial(block, False), carry)
    _, total = block(True, i, carry)
    o_ref[...] = (acc_ref[...] / total).T.astype(jnp.bfloat16)


def attention(cq_all, kv_all, w_uq, w_ukv, pos_all, blk):
    tok = cq_all.shape[0]
    n_blk = tok // blk
    half = ROPE_DIM // 2
    start = jnp.arange(tok, dtype=jnp.int32) - pos_all
    lo = start[::blk] // blk
    clear = jnp.clip((start[blk - 1::blk] + blk - 1) // blk, lo, jnp.arange(n_blk, dtype=jnp.int32))
    inv_freq = 10000.0 ** (-jnp.arange(half, dtype=jnp.float32) / half)
    angles = inv_freq[:, None] * pos_all.astype(jnp.float32)[None, :]
    whole = lambda a: pl.BlockSpec(a.shape, lambda i, *_: (0, 0), pipeline_mode=pl.Buffered(1))
    wq = w_uq.T
    wk = w_ukv[:, :NOPE_DIM]
    wv = w_ukv[:, NOPE_DIM:].T
    lane_blk = lambda r: pl.BlockSpec((r, blk), lambda i, *_: (0, i))
    return pl.pallas_call(
        functools.partial(attn_kernel, blk=blk, n_blk=n_blk),
        name="attention",
        out_shape=jax.ShapeDtypeStruct((tok, VALUE_DIM), jnp.bfloat16),
        grid_spec=pltpu.PrefetchScalarGridSpec(
            num_scalar_prefetch=2,
            grid=(n_blk,),
            in_specs=[
                pl.BlockSpec((blk, cq_all.shape[1]), lambda i, *_: (i, 0)),
                whole(kv_all), whole(wq), whole(wk), whole(wv),
                lane_blk(half), lane_blk(half), lane_blk(1), lane_blk(1),
            ],
            out_specs=pl.BlockSpec((blk, VALUE_DIM), lambda i, *_: (i, 0)),
            scratch_shapes=[
                pltpu.VMEM((tok, 2 * NOPE_DIM), jnp.bfloat16),
                pltpu.VMEM((VALUE_DIM, tok), jnp.bfloat16),
                pltpu.VMEM((2 * NOPE_DIM, blk), jnp.bfloat16),
                pltpu.VMEM((VALUE_DIM, blk), jnp.float32),
            ],
        ),
        cost_estimate=pl.CostEstimate(flops=10_000_000_000, bytes_accessed=14_000_000, transcendentals=9_000_000),
        compiler_params=pltpu.CompilerParams(dimension_semantics=("arbitrary",), vmem_limit_bytes=48 << 20),
    )(lo, clear, cq_all, kv_all, wq, wk, wv, jnp.cos(angles), jnp.sin(angles), start[None, :], pos_all[None, :])


def ffn_kernel(y_ref, g_ref, *rest, dim, pad, sub, tile_n):
    n_wt = 10
    weights = rest[:n_wt]
    (out_ref, ybuf, wgu, wdn, hbuf, gubuf, part, far_l, far_r, in_l, in_r, far2_l, far2_r, in2_l, in2_r,
     w_sem, ag_send, ag_recv, rs_send, rs_recv) = rest[n_wt:]
    me = lax.axis_index("sp")
    core = lax.rem(me, CORES)
    x = lax.rem(me // CORES, RING)
    y = lax.rem(me // (CORES * RING), RING)
    z = me // (CORES * RING * RING)

    def device(yy, xx):
        return {"sp": ((z * RING + yy) * RING + xx) * CORES + core}

    x_up, x_dn = device(y, lax.rem(x + 1, RING)), device(y, lax.rem(x + RING - 1, RING))
    y_up, y_dn = device(lax.rem(y + 1, RING), x), device(lax.rem(y + RING - 1, RING), x)
    up1, dn1, up2, dn2 = (x_up, y_up), (x_dn, y_dn), (y_up, x_up), (y_dn, x_dn)

    barrier = pltpu.get_barrier_semaphore()
    for nb in (x_up, x_dn, y_up, y_dn):
        pl.semaphore_signal(barrier, inc=1, device_id=nb, device_id_type=pl.DeviceIdType.MESH)

    w_copies = []

    def fetch(src, dst):
        cp = pltpu.make_async_copy(src, dst, w_sem.at[len(w_copies)])
        cp.start()
        w_copies.append(cp)

    cut = weights[3].shape[0]
    for side in range(2):
        own, left, right, f0, f1 = weights[5 * side:5 * side + 5]
        for n, blk in enumerate((own, left, right)):
            r = (4 * side + n) * pad
            fetch(blk.at[0:pad], wgu.at[r:r + pad])
            fetch(blk.at[pad:2 * pad], wgu.at[8 * pad + r:8 * pad + r + pad])
            fetch(blk.at[2 * pad:], wdn.at[r:r + pad])
        r = (4 * side + 3) * pad
        fetch(f0.at[0:pad], wgu.at[r:r + pad])
        fetch(f0.at[pad:cut], wgu.at[8 * pad + r:8 * pad + r + cut - pad])
        fetch(f1.at[0:2 * pad - cut], wgu.at[8 * pad + r + cut - pad:8 * pad + r + pad])
        fetch(f1.at[2 * pad - cut:], wdn.at[r:r + pad])

    for h in range(2):
        ybuf[h, 0] = y_ref[h * sub:(h + 1) * sub, :]
    pl.semaphore_wait(barrier, 4)

    cols = (slice(0, dim // 2), slice(dim // 2, dim))
    ag_copies = {}
    ag_n = [0]

    def ag_send_to(h, src_slot, dst_slot, dev, col=None):
        c = slice(None) if col is None else cols[col]
        key = (h, dst_slot, col)
        rsem = dst_slot if col != 1 else RING * RING
        cp = pltpu.make_async_remote_copy(
            src_ref=ybuf.at[h, src_slot, :, c], dst_ref=ybuf.at[h, dst_slot, :, c],
            send_sem=ag_send.at[ag_n[0]], recv_sem=ag_recv.at[h, rsem],
            device_id=dev, device_id_type=pl.DeviceIdType.MESH)
        ag_n[0] += 1
        cp.start()
        ag_copies[key] = cp

    far = 2
    for h in range(2):
        ag_send_to(h, 0, 3 * RING, up1[h])
        ag_send_to(h, 0, 1 * RING, dn1[h])
    for h in range(2):
        ag_send_to(h, 0, 3, up2[h])
        ag_send_to(h, 0, 1, dn2[h])
    for h in range(2):
        ag_copies[(h, 3 * RING, None)].wait_recv()
        ag_send_to(h, 3 * RING, far * RING, up1[h], 0)
        ag_copies[(h, 1 * RING, None)].wait_recv()
        ag_send_to(h, 1 * RING, far * RING, dn1[h], 1)
        for d1 in (3, 1):
            ag_send_to(h, d1 * RING, d1 * RING + 3, up2[h])
            ag_send_to(h, d1 * RING, d1 * RING + 1, dn2[h])
    for h in range(2):
        ag_copies[(h, far * RING, 0)].wait_recv()
        ag_copies[(h, far * RING, 1)].wait_recv()
        ag_send_to(h, far * RING, far * RING + 3, up2[h])
        ag_send_to(h, far * RING, far * RING + 1, dn2[h])
    for d1, d2, dev in ((0, 3, up2), (3, 3, up2), (1, 1, dn2), (2, 1, dn2)):
        for h in range(2):
            ag_copies[(h, d1 * RING + d2, None)].wait_recv()
            ag_send_to(h, d1 * RING + d2, d1 * RING + far, dev[h])
    for d1, d2 in ((0, 1), (3, 1), (1, 3), (2, 3), (0, 2), (3, 2), (1, 2), (2, 2)):
        for h in range(2):
            ag_copies[(h, d1 * RING + d2, None)].wait_recv()

    for cp in w_copies:
        cp.wait()

    rows = 2 * RING * sub
    nt = (((1,), (1,)), ((), ()))
    ff_pad = 8 * pad

    def compute(d1):
        for h in range(2):
            for d2 in range(RING):
                v = ybuf[h, d1 * RING + d2].astype(jnp.float32)
                mean_sq = jnp.mean(v * v, axis=-1, keepdims=True)
                r = (h * RING + d2) * sub
                hbuf[r:r + sub, :] = (v * lax.rsqrt(mean_sq + 1e-6) * g_ref[...].astype(jnp.float32)).astype(jnp.bfloat16)
        n_gu = gubuf.shape[1] // tile_n

        @pl.loop(0, n_gu)
        def _(j):
            c = pl.ds(pl.multiple_of(j * tile_n, tile_n), tile_n)
            gubuf[:, c] = lax.dot_general(hbuf[...], wgu[c, :], nt, preferred_element_type=jnp.float32)

        gate = gubuf[:, :ff_pad]
        act = (gate * jax.nn.sigmoid(gate) * gubuf[:, ff_pad:]).astype(jnp.bfloat16)
        wide = dim // 7 if dim % (7 * 128) == 0 else dim
        for j in range(dim // wide):
            c = slice(j * wide, (j + 1) * wide)
            res = jnp.dot(act, wdn[:, c], preferred_element_type=jnp.float32)
            for h in range(2):
                for d2 in range(RING):
                    r = (h * RING + d2) * sub
                    part[h, d1 * RING + d2, :, c] = res[r:r + sub]

    rs_copies = {}
    rs_n = [0]

    def rs_send_to(key, src, dst, dev):
        cp = pltpu.make_async_remote_copy(
            src_ref=src, dst_ref=dst, send_sem=rs_send.at[rs_n[0]], recv_sem=rs_recv.at[rs_n[0]],
            device_id=dev, device_id_type=pl.DeviceIdType.MESH)
        rs_n[0] += 1
        cp.start()
        rs_copies[key] = cp

    order = (2, 1, 3, 0)
    compute(far)
    for d2 in order:
        for h in range(2):
            rs_send_to(("fl", h, d2), part.at[h, far * RING + d2, :, cols[0]], far_l.at[h, d2], up1[h])
            rs_send_to(("fr", h, d2), part.at[h, far * RING + d2, :, cols[1]], far_r.at[h, d2], dn1[h])
    compute(1)
    compute(3)
    for d2 in order:
        for h in range(2):
            rs_copies[("fl", h, d2)].wait_recv()
            part[h, RING + d2, :, cols[0]] += far_l[h, d2]
            rs_send_to(("il", h, d2), part.at[h, RING + d2], in_l.at[h, d2], up1[h])
            rs_copies[("fr", h, d2)].wait_recv()
            part[h, 3 * RING + d2, :, cols[1]] += far_r[h, d2]
            rs_send_to(("ir", h, d2), part.at[h, 3 * RING + d2], in_r.at[h, d2], dn1[h])
    compute(0)

    def first_sum(h, d2):
        rs_copies[("il", h, d2)].wait_recv()
        rs_copies[("ir", h, d2)].wait_recv()
        part[h, d2] = part[h, d2] + in_l[h, d2] + in_r[h, d2]

    for h in range(2):
        first_sum(h, 2)
        rs_send_to(("gl", h), part.at[h, 2, :, cols[0]], far2_l.at[h], up2[h])
        rs_send_to(("gr", h), part.at[h, 2, :, cols[1]], far2_r.at[h], dn2[h])
    for h in range(2):
        first_sum(h, 1)
        rs_copies[("gl", h)].wait_recv()
        part[h, 1, :, cols[0]] += far2_l[h]
        rs_send_to(("jl", h), part.at[h, 1], in2_l.at[h], up2[h])
        first_sum(h, 3)
        rs_copies[("gr", h)].wait_recv()
        part[h, 3, :, cols[1]] += far2_r[h]
        rs_send_to(("jr", h), part.at[h, 3], in2_r.at[h], dn2[h])
    for h in range(2):
        first_sum(h, 0)
        rs_copies[("jl", h)].wait_recv()
        rs_copies[("jr", h)].wait_recv()
        total = part[h, 0] + in2_l[h] + in2_r[h]
        out_ref[h * sub:(h + 1) * sub, :] = (ybuf[h, 0].astype(jnp.float32) + total).astype(jnp.bfloat16)
    for cp in list(ag_copies.values()) + list(rs_copies.values()):
        cp.wait_send()


def ffn(y_own, g_ffn, weights, pad):
    rows, dim = y_own.shape
    sub = rows // 2
    chunk = 2 * RING * sub
    f32, bf16 = jnp.float32, jnp.bfloat16
    vm = pl.BlockSpec(memory_space=pltpu.VMEM)
    hbm = pl.BlockSpec(memory_space=pl.ANY)
    half = dim // 2
    return pl.pallas_call(
        functools.partial(ffn_kernel, dim=dim, pad=pad, sub=sub, tile_n=256 if (16 * pad) % 256 == 0 else 16 * pad),
        name="ffn",
        out_shape=jax.ShapeDtypeStruct((rows, dim), bf16),
        in_specs=[vm, vm] + [hbm] * 10,
        out_specs=vm,
        scratch_shapes=[
            pltpu.VMEM((2, RING * RING, sub, dim), bf16),
            pltpu.VMEM((16 * pad, dim), bf16),
            pltpu.VMEM((8 * pad, dim), bf16),
            pltpu.VMEM((chunk, dim), bf16),
            pltpu.VMEM((chunk, 16 * pad), f32),
            pltpu.VMEM((2, RING * RING, sub, dim), f32),
            pltpu.VMEM((2, RING, sub, half), f32),
            pltpu.VMEM((2, RING, sub, half), f32),
            pltpu.VMEM((2, RING, sub, dim), f32),
            pltpu.VMEM((2, RING, sub, dim), f32),
            pltpu.VMEM((2, sub, half), f32),
            pltpu.VMEM((2, sub, half), f32),
            pltpu.VMEM((2, sub, dim), f32),
            pltpu.VMEM((2, sub, dim), f32),
            pltpu.SemaphoreType.DMA((26,)),
            pltpu.SemaphoreType.DMA((32,)),
            pltpu.SemaphoreType.DMA((2, RING * RING + 1)),
            pltpu.SemaphoreType.DMA((40,)),
            pltpu.SemaphoreType.DMA((40,)),
        ],
        cost_estimate=pl.CostEstimate(flops=7_000_000_000, bytes_accessed=14_000_000, transcendentals=0),
        compiler_params=pltpu.CompilerParams(collective_id=1, has_side_effects=True, vmem_limit_bytes=56 << 20),
    )(y_own, g_ffn[None, :], *weights)


def gather_weights(w_gate, w_up, w_down, group_size):
    cols = w_down.shape[0]
    pad = -(-cols // 16) * 16
    wide = lambda w: jnp.pad(w, ((0, pad - cols), (0, 0)))
    own = jnp.concatenate([wide(w_gate.T), wide(w_up.T), wide(w_down)], axis=0)
    cut = pad + (pad // 2) // 16 * 16
    plane = RING * RING * CORES
    up = [(d, (d + plane) % group_size) for d in range(group_size)]
    down = [(d, (d - plane) % group_size) for d in range(group_size)]
    swap = [(d, d ^ 1) for d in range(group_size)]
    left = lax.ppermute(own, 'sp', up)
    right = lax.ppermute(own, 'sp', down)
    far0 = lax.ppermute(left[:cut], 'sp', up)
    far1 = lax.ppermute(right[cut:], 'sp', down)
    mine = [own, left, right, far0, far1]
    return mine + [lax.ppermute(w, 'sp', swap) for w in mine], pad


def solution(mesh):
    group_size = mesh.shape['sp']
    tok_spec = P(('dp', 'sp'), None)
    row_spec = P(('dp', 'sp'))
    full_spec = P()
    col_spec = P(None, 'sp')

    def device_fn(x_blk, seg_blk, pos_blk, w_dq, g_q, w_uq, w_dkv, g_kv, w_ukv, w_o, g_ffn, w_gate, w_up, w_down):
        blk_len = x_blk.shape[0]
        tok_total = blk_len * group_size
        weights, pad = gather_weights(w_gate, w_up, w_down, group_size)

        q_lin = jnp.dot(x_blk, w_dq, preferred_element_type=jnp.float32)
        c_q = rms_norm(q_lin, g_q).astype(jnp.bfloat16)
        kv_lin = jnp.dot(x_blk, w_dkv, preferred_element_type=jnp.float32)
        c_kv = rms_norm(kv_lin[:, :KV_LATENT], g_kv).astype(jnp.bfloat16)
        k_rope = apply_rope(kv_lin[:, KV_LATENT:], pos_blk).astype(jnp.bfloat16)
        pos_hi = (pos_blk // 64).astype(jnp.bfloat16)[:, None]
        pos_lo = (pos_blk % 64).astype(jnp.bfloat16)[:, None]
        spare = jnp.zeros((blk_len, NOPE_DIM - ROPE_DIM - 2), jnp.bfloat16)
        kv_blk = jnp.concatenate([c_kv, k_rope, pos_hi, pos_lo, spare], axis=1)
        cq_all = lax.all_gather(c_q, 'sp', axis=0, tiled=True)
        kv_all = lax.all_gather(kv_blk, 'sp', axis=0, tiled=True)
        at = KV_LATENT + ROPE_DIM
        pos_all = kv_all[:, at].astype(jnp.int32) * 64 + kv_all[:, at + 1].astype(jnp.int32)

        o_loc = attention(cq_all, kv_all, w_uq, w_ukv, pos_all, min(512, tok_total))
        o_tok = lax.all_to_all(o_loc, 'sp', 0, 1, tiled=True)
        y_att = jnp.dot(o_tok, w_o, preferred_element_type=jnp.float32).astype(jnp.bfloat16)
        return ffn(y_att, g_ffn, weights, pad)

    return jax.shard_map(device_fn, mesh=mesh, in_specs=(tok_spec, row_spec, row_spec, full_spec, full_spec, col_spec, full_spec, full_spec, col_spec, full_spec, full_spec, col_spec, col_spec, P('sp', None)), out_specs=tok_spec, check_vma=False)
```

time: 1280 us -> 341 us (0.27)
  waiting for transfers between devices: 880 us -> 148 us
  matrix products: 209 us -> 46.8 us
  Pallas kernels: 0 us -> 106 us
  blocking collectives: 102 us -> 0 us
  loops' own time: 21.6 us -> 0 us
  local copies, waits for them, and re-layouts: 26.5 us -> 8.53 us
  other arithmetic: 21.7 us -> 6.95 us
    reduce_scatter x1 -> x0, waiting for transfers between devices: 740 us -> none  [device_fn(): ffn_out = lax.psum_scatter(part_sum, 'sp', scatter_dimension=0, tiled=True)]
    dot_general x102 -> x2, matrix products: 170 us -> 7.14 us  [the longest x1 3.71 us: device_fn(): q_lin = jnp.dot(x_blk, w_dq, preferred_element_type=jnp.float32)]
    pallas_call x0 -> x2, Pallas kernels: none -> 106 us  [the longest x1 72.4 us: ffn(): pl.pallas_call(functools.partial(ffn_kernel, dim=dim, pad=pad, sub=sub, t...]
    unnamed x1 -> x0, blocking collectives: 68.4 us -> none
    all_gather x1, waiting for transfers between devices: 25.6 us -> 63.7 us  [device_fn(): cq_all = lax.all_gather(c_q, 'sp', axis=0, tiled=True)]
    all_gather x2 -> x1, waiting for transfers between devices: 95.5 us -> 59.8 us  [device_fn(): kv_all = lax.all_gather(kv_blk, 'sp', axis=0, tiled=True)]
    all_gather x1 -> x0, blocking collectives: 34.1 us -> none  [device_fn(): kr_all = lax.all_gather(k_rope, 'sp', axis=0, tiled=True)]
    ppermute x0 -> x9, waiting for transfers between devices: none -> 24.6 us  [the longest x1 24.6 us: gather_weights(): far0 = lax.ppermute(left[:cut], 'sp', up)]
  transfers between devices with their start and end apart: 5 -> 12, of which waited for: 4 -> 3; matrix products, arithmetic and copies ran while one was open for 1% -> 16% of each run, Pallas kernels for 0% -> 10%
where the time goes in v1:
time: 341 us; the launch traced here: 345 us
  waiting for transfers between devices  148 us (43%)
  Pallas kernels  106 us (31%)
  matrix products  46.8 us (14%)
  starting transfers between devices  14.5 us (4%)
  between operations  13.7 us (4%)
  local copies, waits for them, and re-layouts  8.53 us (3%)
  other arithmetic  6.95 us (2%)
    pallas_call x1, Pallas kernels, ffn(): pl.pallas_call(functools.partial(ffn_kernel, dim=dim, pad=pad, sub=sub, t...  72.4 us
    all_gather x1, waiting for transfers between devices, device_fn(): cq_all = lax.all_gather(c_q, 'sp', axis=0, tiled=True)  63.7 us
    all_gather x1, waiting for transfers between devices, device_fn(): kv_all = lax.all_gather(kv_blk, 'sp', axis=0, tiled=True)  59.8 us
    dot_general x1, matrix products, device_fn(): jnp.dot(o_tok, w_o, preferred_element_type=jnp.float32).astype(jnp.bfloat16)  39.7 us
    pallas_call x1, Pallas kernels, attention(): pl.pallas_call(functools.partial(attn_kernel, blk=blk, n_blk=n_blk), name...  33.9 us
    ppermute x1, waiting for transfers between devices, gather_weights(): far0 = lax.ppermute(left[:cut], 'sp', up)  24.6 us
  transfers between devices with their start and end apart: 12, of which 3 were waited for; matrix products, arithmetic and copies ran while one was open for 16% of the time, Pallas kernels for 10%

profile of v1, /device:TPU:0, one launch (start us, length us, event | category | flops | bytes accessed | tf_op | source)
XLA Modules:
  0.0 345.0 jit_solution(1062891451680368469)
XLA Ops:
  6.5 0.0 copy-start
  6.5 0.0 all-gather.3.cloned.1.call-start
  6.6 0.7 fusion.17
  7.3 0.2 copy-done
  7.5 3.4 fusion.19
  10.9 0.0 copy-start.3
  11.0 0.0 copy-start.4
  11.0 0.0 copy-start.5
  11.0 0.1 multiply_reduce_fusion.1
  11.1 0.0 copy-done.8
  11.1 0.1 copy.25
  11.2 0.1 copy.26
  11.3 0.1 fusion.15
  11.5 0.1 multiply_convert_fusion.1
  11.6 0.7 concatenate.9
  12.3 0.0 all-gather.3.cloned.1.call-update
  12.3 0.0 all-gather.5.cloned.1.call-start
  12.3 0.0 copy-done.7
  12.4 3.7 %multiply_reduce_fusion = (f32[32]{0:T(128)S(1)}, f32[32,768]{1,0:T(8,128)S(1)}) fusion(bf16[32,3584]{1,0:T(8,128)(2,1)S(1)} %copy-done, bf16[3584,768]{1,0:T(8,128)(2,1)} %param.16), kind=kOutput, calls=%fused_computation.17 | convolution fusion | flops 176209888 | bytes 5832832 | tf_op jit(solution)/shard_map/dot_general | solution.py:383
  16.1 0.7 multiply_convert_fusion
  16.8 0.0 all-gather.5.cloned.1.call-update
  16.8 0.0 copy-done.3
  16.8 0.0 copy-done.4
  16.9 0.1 fusion.5.rest_0_
  17.0 0.0 copy-start.2
  17.0 4.2 %collective-permute-start.1 = (bf16[240,3584]{1,0:T(8,128)(2,1)S(1)}, bf16[240,3584]{1,0:T(8,128)(2,1)}, u32[]{:S(2)}, u32[]{:S(2)}) collective-permute-start(bf16[240,3584]{1,0:T(8,128)(2,1)S(1)} %fusion.5.rest_0_), channel_id=1, source_target_pairs={{0,96},{1,97},{2,98},{3,99},{4,100},{5,101},{6,102},{7,103},{8,104... | collective-permute-start | bytes 5160968 | tf_op jit(solution)/shard_map/ppermute | solution.py:364
  21.3 0.0 collective-permute-start
  21.3 1.0 constant_dynamic-slice_fusion.1
  22.3 0.1 copy.34
  22.4 1.2 constant_dynamic-slice_fusion.2
  23.6 0.2 copy.31
  23.8 59.8 %all-gather.3.cloned.1.call-done.kv_ref = bf16[4096,640]{1,0:T(8,128)(2,1)} async-done(((bf16[32,640]{1,0:T(8,128)(2,1)}), bf16[4096,640]{1,0:T(8,128)(2,1)}) %all-gather.3.cloned.1.call-update) | async-done | bytes 5242896 | tf_op jit(solution)/shard_map/all_gather | solution.py:393
  83.5 3.1 add_reduce_fusion
  86.6 1.9 multiply_sine_fusion
  88.6 0.1 slice.41
  88.7 0.1 slice.42
  88.8 63.7 %all-gather.5.cloned.1.call-done.cq_ref = bf16[4096,768]{1,0:T(8,128)(2,1)} async-done(((bf16[32,768]{1,0:T(8,128)(2,1)}), bf16[4096,768]{1,0:T(8,128)(2,1)}) %all-gather.5.cloned.1.call-update) | async-done | bytes 6291472 | tf_op jit(solution)/shard_map/all_gather | solution.py:392
  152.5 33.9 %attention.1 = bf16[4096,128]{1,0:T(8,128)(2,1)} custom-call(s32[8]{0:T(128)S(1)} %get-tuple-element.6.lo_ref, s32[8]{0:T(128)S(1)} %get-tuple-element.5.clear_ref, bf16[4096,768]{1,0:T(8,128)(2,1)} %all-gather.5.cloned.1.call-done.cq_ref, bf16[4096,640]{1,0:T(8,128)(2,1)} %all-gather.3.cloned.1.call-done.kv_ref, bf16[192,768]{1,0:T(8,128)(2,1)S(1)} %bitcast.23, ...), custom_call_target="tpu_custom_call" | custom-call | flops 10000000000 | bytes 14000000 | tf_op jit(solution)/shard_map/attention/pallas_call | solution.py:108
  186.4 6.1 %all-to-all-start = ((bf16[128,32,128]{2,1,0:T(8,128)(2,1)}), bf16[128,32,128]{2,1,0:T(8,128)(2,1)S(1)}, u32[]{:S(2)}, u32[]{:S(2)}) async-start(bf16[128,32,128]{2,1,0:T(8,128)(2,1)} %bitcast.4), calls=%async_computation | async-start | bytes 2097152 | tf_op jit(solution)/shard_map/all_to_all | solution.py:398
  192.6 0.0 collective-permute-done.1.rest_2_
  192.6 1.2 slice.53
  193.8 2.9 collective-permute-start.3
  196.7 0.0 collective-permute-done.rest_1_
  196.7 1.2 slice.52
  197.9 0.1 collective-permute-start.2
  198.0 0.0 copy-done.2
  198.0 0.1 collective-permute-start.4
  198.1 0.6 broadcast_in_dim.11.g_ref
  198.7 0.5 collective-permute-start.5
  199.2 0.0 collective-permute-start.6
  199.2 24.6 %collective-permute-done.2.rest_3_ = bf16[112,3584]{1,0:T(8,128)(2,1)} collective-permute-done((bf16[112,3584]{1,0:T(8,128)(2,1)S(1)}, bf16[112,3584]{1,0:T(8,128)(2,1)}, u32[]{:S(2)}, u32[]{:S(2)}) %collective-permute-start.2) | collective-permute-done | bytes 802848 | tf_op jit(solution)/shard_map/ppermute | solution.py:365
  223.8 0.0 collective-permute-start.7
  223.9 0.0 collective-permute-done.3.rest_4_
  223.9 0.5 collective-permute-start.8
  224.4 0.0 all-to-all-done
  224.4 39.7 %convolution_convert_fusion.y_ref = bf16[32,3584]{1,0:T(8,128)(2,1)} fusion(bf16[16384,3584]{1,0:T(8,128)(2,1)} %param.22, bf16[128,32,128]{2,1,0:T(8,128)(2,1)S(1)} %all-to-all-done), kind=kOutput, calls=%fused_computation.2 | convolution fusion | flops 3758211072 | bytes 118718464 | tf_op jit(solution)/shard_map/dot_general | solution.py:399
  264.0 0.0 collective-permute-done.4.rest_5_
  264.0 0.0 collective-permute-done.7.rest_8_
  264.0 0.0 collective-permute-done.5.rest_6_
  264.1 0.0 collective-permute-done.6.rest_7_
  264.1 0.0 collective-permute-done.8.rest_9_
  264.1 0.0 copy-start.1
  264.1 72.4 %ffn.1 = bf16[32,3584]{1,0:T(8,128)(2,1)} custom-call(bf16[32,3584]{1,0:T(8,128)(2,1)} %convolution_convert_fusion.y_ref, bf16[1,3584]{1,0:T(2,128)(2,1)} %broadcast_in_dim.11.g_ref, bf16[240,3584]{1,0:T(8,128)(2,1)} %copy-done.2, bf16[240,3584]{1,0:T(8,128)(2,1)} %collective-permute-done.rest_1_, bf16[240,3584]{1,0:T(8,128)(2,1)} %collective-permute-done.1.rest_2_, ...), custom_call_target="tpu_custom_call" | custom-call | flops 7000000000 | bytes 14000000 | tf_op jit(solution)/shard_map/ffn/pallas_call | solution.py:321
  336.5 1.6 copy.41
  (15 shorter events, 0.1 us)
Async XLA Ops:
  6.5 1.0 copy-start
  6.5 4.6 %copy-start.8 = (bf16[512]{0:T(512)(128)(2,1)S(1)}, bf16[512]{0:T(512)(128)(2,1)}, u32[]{:S(2)}) copy-start(bf16[512]{0:T(512)(128)(2,1)} %param.20) | copy-start | bytes 3076
  6.5 5.8 %copy-start.7 = (bf16[768]{0:T(1024)(128)(2,1)S(1)}, bf16[768]{0:T(1024)(128)(2,1)}, u32[]{:S(2)}) copy-start(bf16[768]{0:T(1024)(128)(2,1)} %param.17) | copy-start | bytes 4612
  6.5 77.0 %all-gather.3.cloned.1.call-start = ((), (), s32[]{:S(2)}) async-start(), calls=%async_computation.1 | async-start | bytes 5283840 | tf_op jit(solution)/shard_map/all_gather | solution.py:393
  10.9 5.9 %copy-start.3 = (bf16[72,3584]{1,0:T(8,128)(2,1)S(1)}, bf16[72,3584]{1,0:T(8,128)(2,1)}, u32[]{:S(2)}) copy-start(bf16[72,3584]{1,0:T(8,128)(2,1)} %param.26) | copy-start | bytes 1548292
  11.0 5.9 %copy-start.4 = (bf16[3584,72]{0,1:T(8,128)(2,1)S(1)}, bf16[3584,72]{0,1:T(8,128)(2,1)}, u32[]{:S(2)}) copy-start(bf16[3584,72]{0,1:T(8,128)(2,1)} %param.25) | copy-start | bytes 1548292
  11.0 5.9 %copy-start.5 = (bf16[3584,72]{0,1:T(8,128)(2,1)S(1)}, bf16[3584,72]{0,1:T(8,128)(2,1)}, u32[]{:S(2)}) copy-start(bf16[3584,72]{0,1:T(8,128)(2,1)} %param.24) | copy-start | bytes 1548292
  12.3 140.2 %all-gather.5.cloned.1.call-start = ((), (), s32[]{:S(2)}) async-start(), calls=%async_computation.2 | async-start | bytes 6340608 | tf_op jit(solution)/shard_map/all_gather | solution.py:392
  17.0 181.0 %copy-start.2 = (bf16[240,3584]{1,0:T(8,128)(2,1)}, bf16[240,3584]{1,0:T(8,128)(2,1)S(1)}, u32[]{:S(2)}) copy-start(bf16[240,3584]{1,0:T(8,128)(2,1)S(1)} %fusion.5.rest_0_) | copy-start | bytes 5160964
  17.0 175.6 %collective-permute-start.1 = (bf16[240,3584]{1,0:T(8,128)(2,1)S(1)}, bf16[240,3584]{1,0:T(8,128)(2,1)}, u32[]{:S(2)}, u32[]{:S(2)}) collective-permute-start(bf16[240,3584]{1,0:T(8,128)(2,1)S(1)} %fusion.5.rest_0_), channel_id=1, source_target_pairs={{0,96},{1,97},{2,98},{3,99},{4,100},{5,101},{6,102},{7,103},{8,104... | collective-permute-start | bytes 5160968 | tf_op jit(solution)/shard_map/ppermute | solution.py:364
  21.3 175.5 %collective-permute-start = (bf16[240,3584]{1,0:T(8,128)(2,1)S(1)}, bf16[240,3584]{1,0:T(8,128)(2,1)}, u32[]{:S(2)}, u32[]{:S(2)}) collective-permute-start(bf16[240,3584]{1,0:T(8,128)(2,1)S(1)} %fusion.5.rest_0_), channel_id=1, source_target_pairs={{0,32},{1,33},{2,34},{3,35},{4,36},{5,37},{6,38},{7,39},{8,40},{9,... | collective-permute-start | bytes 5160968 | tf_op jit(solution)/shard_map/ppermute | solution.py:363
  186.4 11.7 %copy-start.6 = (bf16[3584]{0:T(1024)(128)(2,1)S(1)}, bf16[3584]{0:T(1024)(128)(2,1)}, u32[]{:S(2)}) copy-start(bf16[3584]{0:T(1024)(128)(2,1)} %param.23) | copy-start | bytes 21508
  186.4 37.9 %all-to-all-start = ((bf16[128,32,128]{2,1,0:T(8,128)(2,1)}), bf16[128,32,128]{2,1,0:T(8,128)(2,1)S(1)}, u32[]{:S(2)}, u32[]{:S(2)}) async-start(bf16[128,32,128]{2,1,0:T(8,128)(2,1)} %bitcast.4), calls=%async_computation | async-start | bytes 2097152 | tf_op jit(solution)/shard_map/all_to_all | solution.py:398
  193.8 30.0 %collective-permute-start.3 = (bf16[128,3584]{1,0:T(8,128)(2,1)S(1)}, bf16[128,3584]{1,0:T(8,128)(2,1)}, u32[]{:S(2)}, u32[]{:S(2)}) collective-permute-start(bf16[128,3584]{1,0:T(8,128)(2,1)S(1)} %slice.53), channel_id=1, source_target_pairs={{0,96},{1,97},{2,98},{3,99},{4,100},{5,101},{6,102},{7,103},{8,104... | collective-permute-start | bytes 2752520 | tf_op jit(solution)/shard_map/ppermute | solution.py:366
  197.9 25.9 %collective-permute-start.2 = (bf16[112,3584]{1,0:T(8,128)(2,1)S(1)}, bf16[112,3584]{1,0:T(8,128)(2,1)}, u32[]{:S(2)}, u32[]{:S(2)}) collective-permute-start(bf16[112,3584]{1,0:T(8,128)(2,1)S(1)} %slice.52), channel_id=1, source_target_pairs={{0,32},{1,33},{2,34},{3,35},{4,36},{5,37},{6,38},{7,39},{8,40},{9,... | collective-permute-start | bytes 2408456 | tf_op jit(solution)/shard_map/ppermute | solution.py:365
  198.0 66.0 %collective-permute-start.4 = (bf16[240,3584]{1,0:T(8,128)(2,1)S(1)}, bf16[240,3584]{1,0:T(8,128)(2,1)}, u32[]{:S(2)}, u32[]{:S(2)}) collective-permute-start(bf16[240,3584]{1,0:T(8,128)(2,1)S(1)} %fusion.5.rest_0_), channel_id=1, source_target_pairs={{0,1},{1,0},{2,3},{3,2},{4,5},{5,4},{6,7},{7,6},{8,9},{9,8},{10,11... | collective-permute-start | bytes 5160968 | tf_op jit(solution)/shard_map/ppermute | solution.py:368
  198.7 65.3 %collective-permute-start.5 = (bf16[240,3584]{1,0:T(8,128)(2,1)}, bf16[240,3584]{1,0:T(8,128)(2,1)}, u32[]{:S(2)}, u32[]{:S(2)}) collective-permute-start(bf16[240,3584]{1,0:T(8,128)(2,1)} %collective-permute-done.rest_1_), channel_id=1, source_target_pairs={{0,1},{1,0},{2,3},{3,2},{4,5},{5,4},{6,7},{7,6},{8,9},{9,8},{10,11... | collective-permute-start | bytes 5160968 | tf_op jit(solution)/shard_map/ppermute | solution.py:368
  199.2 64.9 %collective-permute-start.6 = (bf16[240,3584]{1,0:T(8,128)(2,1)}, bf16[240,3584]{1,0:T(8,128)(2,1)}, u32[]{:S(2)}, u32[]{:S(2)}) collective-permute-start(bf16[240,3584]{1,0:T(8,128)(2,1)} %collective-permute-done.1.rest_2_), channel_id=1, source_target_pairs={{0,1},{1,0},{2,3},{3,2},{4,5},{5,4},{6,7},{7,6},{8,9},{9,8},{10,11... | collective-permute-start | bytes 5160968 | tf_op jit(solution)/shard_map/ppermute | solution.py:368
  223.8 40.2 %collective-permute-start.7 = (bf16[112,3584]{1,0:T(8,128)(2,1)}, bf16[112,3584]{1,0:T(8,128)(2,1)}, u32[]{:S(2)}, u32[]{:S(2)}) collective-permute-start(bf16[112,3584]{1,0:T(8,128)(2,1)} %collective-permute-done.2.rest_3_), channel_id=1, source_target_pairs={{0,1},{1,0},{2,3},{3,2},{4,5},{5,4},{6,7},{7,6},{8,9},{9,8},{10,11... | collective-permute-start | bytes 2408456 | tf_op jit(solution)/shard_map/ppermute | solution.py:368
  223.9 40.2 %collective-permute-start.8 = (bf16[128,3584]{1,0:T(8,128)(2,1)}, bf16[128,3584]{1,0:T(8,128)(2,1)}, u32[]{:S(2)}, u32[]{:S(2)}) collective-permute-start(bf16[128,3584]{1,0:T(8,128)(2,1)} %collective-permute-done.3.rest_4_), channel_id=1, source_target_pairs={{0,1},{1,0},{2,3},{3,2},{4,5},{5,4},{6,7},{7,6},{8,9},{9,8},{10,11... | collective-permute-start | bytes 2752520 | tf_op jit(solution)/shard_map/ppermute | solution.py:368
  264.1 74.1 %copy-start.1 = (bf16[32,3584]{1,0:T(8,128)(2,1)S(1)}, bf16[32,3584]{1,0:T(8,128)(2,1)}, u32[]{:S(2)}) copy-start(bf16[32,3584]{1,0:T(8,128)(2,1)} %param.14) | copy-start | bytes 688132
Sparse Core Ops, SparseCore 0:
  12.4 71.0 all-gather.2
  86.6 65.8 all-gather.4
